TPU v7x, 32 devices: a whole 2x2x4 slice. The times are simulated.
32 devices in a mesh: grp: 2 (over x), row: 16 (over z, y, core).
Axes of the slice: x: 2, y: 2, z: 4, core: 2. Of those that a mesh axis runs over, the one named last changes fastest.
Arguments:
- kmesh: int32 [32, 3], P(('grp', 'row')), parts along dimension 0, may hold values from 0 to 15
- rcoord: int32 [768, 3], P(('grp', 'row')), parts along dimension 0, may hold values from -8 to 8
- degen: int32 [768], P(('grp', 'row')), parts along dimension 0, may hold values from 1 to 4
- hr_re: float32 [768, 128, 128], P(('grp', 'row')), parts along dimension 0, may hold values from -1.5 to 1.5
- hr_im: float32 [768, 128, 128], P(('grp', 'row')), parts along dimension 0, may hold values from -1.5 to 1.5
Outputs:
- hk_re: float32 [32, 128, 128], P(('grp', 'row')), parts along dimension 0
- hk_im: float32 [32, 128, 128], P(('grp', 'row')), parts along dimension 0
There are 2 independent parts, one for each index of `grp`. A program takes and returns all parts, laid end to end along the dimension named above; each array names one. Nothing has to cross between parts.
All inputs are finite; a program needn't handle non-finite values.
Results may differ from a plain program's by a relative error of at most 0.00007.
Values sent between devices are 32-bit elements; how exact they have to be, the bound alone decides.
No kernel may reach another device: no remote copies, remote signals or barrier semaphores. Data moves between devices by JAX's collectives and lax.ppermute only.
A program may use at most 64 MiB of HBM per device.

v0:
```python
import math
import jax
import jax.numpy as jnp
from jax import lax
from jax.sharding import PartitionSpec as P

MESH = 16


def phase_terms(kblock, coords, inverse, real_flat, imag_flat):
    highest = lax.Precision.HIGHEST
    prod = jnp.sum(kblock[:, None, :] * coords[None, :, :], axis=-1)
    phase = jnp.mod(prod, MESH)
    angle = phase.astype(jnp.float32) * (2.0 * math.pi / MESH)
    cosine = jnp.cos(angle) * inverse[None, :]
    sine = jnp.sin(angle) * inverse[None, :]
    part_re = jnp.dot(
        cosine, real_flat, precision=highest, preferred_element_type=jnp.float32
    ) - jnp.dot(sine, imag_flat, precision=highest, preferred_element_type=jnp.float32)
    part_im = jnp.dot(
        sine, real_flat, precision=highest, preferred_element_type=jnp.float32
    ) + jnp.dot(cosine, imag_flat, precision=highest, preferred_element_type=jnp.float32)
    return (part_re, part_im)


def shards(kmesh, rcoord, degen, hr_re, hr_im):
    width = hr_re.shape[1]
    every_k = lax.all_gather(kmesh, "row", axis=0, tiled=True)
    total_k = every_k.shape[0]
    local_r = hr_re.shape[0]
    real_flat = hr_re.reshape(local_r, -1)
    imag_flat = hr_im.reshape(local_r, -1)
    inverse = 1.0 / degen.astype(jnp.float32)
    part_re, part_im = phase_terms(every_k, rcoord, inverse, real_flat, imag_flat)
    whole = jnp.concatenate([part_re, part_im], axis=1).reshape(total_k, 2, width, width)
    by_rows = lax.psum_scatter(whole, "row", scatter_dimension=2, tiled=True)
    mine = lax.all_to_all(by_rows, "row", split_axis=0, concat_axis=2, tiled=True)
    return (mine[:, 0], mine[:, 1])


def solution(mesh):
    placed = (
        P(("grp", "row"), None),
        P(("grp", "row"), None),
        P(("grp", "row")),
        P(("grp", "row"), None, None),
        P(("grp", "row"), None, None),
    )
    return jax.shard_map(
        shards,
        mesh=mesh,
        in_specs=placed,
        out_specs=(P(("grp", "row"), None, None), P(("grp", "row"), None, None)),
        check_vma=False,
    )
```

profile of v0, /device:TPU:0, one launch (start us, length us, event | category | flops | bytes accessed | tf_op | source)
XLA Modules:
  0.0 121.5 jit_solution(16764732116881558362)
XLA Ops:
  7.2 0.0 copy-start
  7.2 0.0 reduce-scatter.2.cloned.1.call-start
  7.2 0.8 convert_divide_fusion
  8.0 23.3 %all-gather = s32[16,1,3]{2,1,0:T(1,128)S(1)} all-gather(s32[1,1,3]{2,1,0:T(1,128)} %bitcast.35), channel_id=1, replica_groups=mesh['grp'=2,'row'=16] {'row'}, dimensions={0}, use_global_device_ids=true | all-gather | bytes 204 | tf_op jit(solution)/shard_map/all_gather | solution.py:28
  31.3 0.1 copy.15
  31.4 0.8 multiply_reduce_fusion
  32.1 3.3 %fusion.2 = f32[16,16384]{1,0:T(8,128)S(1)} fusion(f32[3,8,128,128]{3,2,1,0:T(8,128)} %bitcast.30, f32[24]{0:T(128)S(1)} %convert_divide_fusion, s32[16,24]{1,0:T(8,128)S(1)} %multiply_reduce_fusion), kind=kOutput, calls=%fused_computation.5 | convolution fusion | flops 75502848 | bytes 2623072 | tf_op jit(solution)/shard_map/dot_general | solution.py:20
  35.4 0.0 copy-done
  35.4 0.0 copy-start.1
  35.4 1.9 %fusion.4 = f32[16,16384]{1,0:T(8,128)S(1)} fusion(f32[3,8,128,128]{3,2,1,0:T(8,128)S(1)} %bitcast.31, f32[24]{0:T(128)S(1)} %convert_divide_fusion, s32[16,24]{1,0:T(8,128)S(1)} %multiply_reduce_fusion), kind=kOutput, calls=%fused_computation.7 | convolution fusion | flops 75502848 | bytes 2623072 | tf_op jit(solution)/shard_map/dot_general | solution.py:17
  37.4 0.0 copy-done.1
  37.4 1.9 %convolution_add_fusion = f32[16,16384]{1,0:T(8,128)S(1)} fusion(f32[16,16384]{1,0:T(8,128)S(1)} %fusion.2, f32[3,8,128,128]{3,2,1,0:T(8,128)S(1)} %bitcast.32, f32[24]{0:T(128)S(1)} %convert_divide_fusion, s32[16,24]{1,0:T(8,128)S(1)} %multiply_reduce_fusion), kind=kOutput, calls=%fused_computation | convolution fusion | flops 75764992 | bytes 3671648 | tf_op jit(solution)/shard_map/dot_general | solution.py:22
  39.3 1.9 %convolution_subtract_fusion = f32[16,16384]{1,0:T(8,128)S(1)} fusion(f32[16,16384]{1,0:T(8,128)S(1)} %fusion.4, f32[3,8,128,128]{3,2,1,0:T(8,128)S(1)} %bitcast.33, f32[24]{0:T(128)S(1)} %convert_divide_fusion, s32[16,24]{1,0:T(8,128)S(1)} %multiply_reduce_fusion), kind=kOutput, calls=%fused_computation.1 | convolution fusion | flops 75764992 | bytes 3671648 | tf_op jit(solution)/shard_map/dot_general | solution.py:19
  41.2 0.1 maximum_bitcast_fusion
  41.4 1.8 %copy.19 = f32[2,8,256,128]{3,2,1,0:T(8,128)} copy(f32[2,8,256,128]{3,1,2,0:T(8,128)S(1)} %maximum_bitcast_fusion) | data formatting | bytes 4194304
  43.1 0.0 reduce-scatter.2.cloned.1.call-update
  43.2 59.2 %reduce-scatter.2.cloned.1.call-done = f32[16,2,8,128]{3,2,1,0:T(8,128)} async-done(((f32[16,2,128,128]{3,2,1,0:T(8,128)}), f32[16,2,8,128]{3,2,1,0:T(8,128)}) %reduce-scatter.2.cloned.1.call-update) | async-done | bytes 131088 | tf_op jit(solution)/shard_map/reduce_scatter | solution.py:36
  102.4 11.6 %all_to_all.18 = f32[16,2,8,128]{3,2,1,0:T(8,128)S(1)} all-to-all(f32[16,2,8,128]{3,2,1,0:T(8,128)} %reduce-scatter.2.cloned.1.call-done), channel_id=1, replica_groups=mesh['grp'=2,'row'=16] {'row'}, dimensions={0} | all-to-all | bytes 262144 | tf_op jit(solution)/shard_map/all_to_all | solution.py:37
  114.0 0.7 slice_bitcast_fusion
  (1 shorter events, 0.0 us)
Async XLA Ops:
  7.2 28.3 %copy-start = (f32[24,128,128]{2,1,0:T(8,128)S(1)}, f32[24,128,128]{2,1,0:T(8,128)}, u32[]{:S(2)}) copy-start(f32[24,128,128]{2,1,0:T(8,128)} %param.8) | copy-start | bytes 4718596
  7.2 95.2 %reduce-scatter.2.cloned.1.call-start = ((), (), s32[]{:S(2)}) async-start(), calls=%async_computation.2 | async-start | bytes 2228224 | tf_op jit(solution)/shard_map/reduce_scatter | solution.py:36
  35.4 1.9 %copy-start.1 = (f32[24,128,128]{2,1,0:T(8,128)S(1)}, f32[24,128,128]{2,1,0:T(8,128)}, u32[]{:S(2)}) copy-start(f32[24,128,128]{2,1,0:T(8,128)} %param.9) | copy-start | bytes 4718596
Sparse Core Ops, SparseCore 0:
  43.3 59.0 reduce-scatter.1
where the time goes:
time: 122 us; the launch traced here: 121 us
  waiting for transfers between devices  59.2 us (49%)
  blocking collectives  34.9 us (29%)
  between operations  14.1 us (12%)
  matrix products  9.08 us (7%)
  local copies, waits for them, and re-layouts  2.51 us (2%)
  other arithmetic  1.66 us (1%)
    reduce_scatter x1, waiting for transfers between devices, shards(): by_rows = lax.psum_scatter(whole, 'row', scatter_dimension=2, tiled=True)  59.2 us
    all_gather x1, blocking collectives, shards(): every_k = lax.all_gather(kmesh, 'row', axis=0, tiled=True)  23.3 us
    all_to_all x1, blocking collectives, shards(): lax.all_to_all(by_rows, 'row', split_axis=0, concat_axis=2, tiled=True)  11.6 us
    dot_general x1, matrix products, phase_terms(): jnp.dot(sine, real_flat, precision=highest, preferred_element_type=jnp.fl...  3.3 us
  transfers between devices with their start and end apart: 1, of which 1 were waited for; matrix products, arithmetic and copies ran while one was open for 0% of the time, Pallas kernels for 0%

commit v1 on v0

--- a/solution.py
+++ b/solution.py
@@ -34,7 +34,10 @@
     part_re, part_im = phase_terms(every_k, rcoord, inverse, real_flat, imag_flat)
     whole = jnp.concatenate([part_re, part_im], axis=1).reshape(total_k, 2, width, width)
     by_rows = lax.psum_scatter(whole, "row", scatter_dimension=2, tiled=True)
-    mine = lax.all_to_all(by_rows, "row", split_axis=0, concat_axis=2, tiled=True)
+    mine = jnp.concatenate(
+        lax.all_to_all(jnp.stack(jnp.split(by_rows, lax.axis_size("row"), axis=0)), "row", 0, 0),
+        axis=2,
+    )
     return (mine[:, 0], mine[:, 1])
 
 

time: 122 us -> 134 us (1.098)
  local copies, waits for them, and re-layouts: 2.51 us -> 13.7 us
    unnamed x5 -> x20, local copies, waits for them, and re-layouts: 1.76 us -> 12.2 us
where the time goes in v1:
time: 134 us; the launch traced here: 132 us
  waiting for transfers between devices  59.2 us (44%)
  blocking collectives  34.7 us (26%)
  between operations  14.1 us (11%)
  local copies, waits for them, and re-layouts  13.7 us (10%)
  matrix products  9.08 us (7%)
  other arithmetic  1.66 us (1%)
    reduce_scatter x1, waiting for transfers between devices, shards(): by_rows = lax.psum_scatter(whole, 'row', scatter_dimension=2, tiled=True)  59.2 us
    all_gather x1, blocking collectives, shards(): every_k = lax.all_gather(kmesh, 'row', axis=0, tiled=True)  23.3 us
    unnamed x20, local copies, waits for them, and re-layouts  12.2 us
    all_to_all x1, blocking collectives, shards(): lax.all_to_all(jnp.stack(jnp.split(by_rows, lax.axis_size('row'), axis=0)...  11.4 us
    dot_general x1, matrix products, phase_terms(): jnp.dot(sine, real_flat, precision=highest, preferred_element_type=jnp.fl...  3.3 us
  transfers between devices with their start and end apart: 1, of which 1 were waited for; matrix products, arithmetic and copies ran while one was open for 0% of the time, Pallas kernels for 0%

profile of v1, /device:TPU:0, one launch (start us, length us, event | category | flops | bytes accessed | tf_op | source)
XLA Modules:
  0.0 132.4 jit_solution(6939908510027072813)
XLA Ops:
  7.2 0.0 copy-start
  7.2 0.0 reduce-scatter.2.cloned.1.call-start
  7.2 0.8 convert_divide_fusion
  8.0 23.3 %all-gather = s32[16,1,3]{2,1,0:T(1,128)S(1)} all-gather(s32[1,1,3]{2,1,0:T(1,128)} %bitcast.97), channel_id=1, replica_groups=mesh['grp'=2,'row'=16] {'row'}, dimensions={0}, use_global_device_ids=true | all-gather | bytes 204 | tf_op jit(solution)/shard_map/all_gather | solution.py:28
  31.3 0.1 copy.15
  31.4 0.8 multiply_reduce_fusion
  32.1 3.3 %fusion.2 = f32[16,16384]{1,0:T(8,128)S(1)} fusion(f32[3,8,128,128]{3,2,1,0:T(8,128)} %bitcast.92, f32[24]{0:T(128)S(1)} %convert_divide_fusion, s32[16,24]{1,0:T(8,128)S(1)} %multiply_reduce_fusion), kind=kOutput, calls=%fused_computation.5 | convolution fusion | flops 75502848 | bytes 2623072 | tf_op jit(solution)/shard_map/dot_general | solution.py:20
  35.4 1.9 %fusion.4 = f32[16,16384]{1,0:T(8,128)S(1)} fusion(f32[3,8,128,128]{3,2,1,0:T(8,128)S(1)} %bitcast.93, f32[24]{0:T(128)S(1)} %convert_divide_fusion, s32[16,24]{1,0:T(8,128)S(1)} %multiply_reduce_fusion), kind=kOutput, calls=%fused_computation.7 | convolution fusion | flops 75502848 | bytes 2623072 | tf_op jit(solution)/shard_map/dot_general | solution.py:17
  37.4 1.9 %convolution_add_fusion = f32[16,16384]{1,0:T(8,128)S(1)} fusion(f32[16,16384]{1,0:T(8,128)S(1)} %fusion.2, f32[3,8,128,128]{3,2,1,0:T(8,128)S(1)} %bitcast.94, f32[24]{0:T(128)S(1)} %convert_divide_fusion, s32[16,24]{1,0:T(8,128)S(1)} %multiply_reduce_fusion), kind=kOutput, calls=%fused_computation | convolution fusion | flops 75764992 | bytes 3671648 | tf_op jit(solution)/shard_map/dot_general | solution.py:22
  39.3 1.9 %convolution_subtract_fusion = f32[16,16384]{1,0:T(8,128)S(1)} fusion(f32[16,16384]{1,0:T(8,128)S(1)} %fusion.4, f32[3,8,128,128]{3,2,1,0:T(8,128)S(1)} %bitcast.95, f32[24]{0:T(128)S(1)} %convert_divide_fusion, s32[16,24]{1,0:T(8,128)S(1)} %multiply_reduce_fusion), kind=kOutput, calls=%fused_computation.1 | convolution fusion | flops 75764992 | bytes 3671648 | tf_op jit(solution)/shard_map/dot_general | solution.py:19
  41.2 0.1 maximum_bitcast_fusion
  41.4 1.8 %copy.19 = f32[2,8,256,128]{3,2,1,0:T(8,128)} copy(f32[2,8,256,128]{3,1,2,0:T(8,128)S(1)} %maximum_bitcast_fusion) | data formatting | bytes 4194304
  43.1 0.0 reduce-scatter.2.cloned.1.call-update
  43.2 59.2 %reduce-scatter.2.cloned.1.call-done = f32[16,2,8,128]{3,2,1,0:T(8,128)} async-done(((f32[16,2,128,128]{3,2,1,0:T(8,128)}), f32[16,2,8,128]{3,2,1,0:T(8,128)}) %reduce-scatter.2.cloned.1.call-update) | async-done | bytes 131088 | tf_op jit(solution)/shard_map/reduce_scatter | solution.py:36
  102.4 0.7 constant_dynamic-update-slice_fusion.15
  103.1 0.7 constant_dynamic-update-slice_fusion.14
  103.8 0.7 constant_dynamic-update-slice_fusion.13
  104.5 0.7 constant_dynamic-update-slice_fusion.12
  105.2 0.7 constant_dynamic-update-slice_fusion.11
  105.9 0.7 constant_dynamic-update-slice_fusion.10
  106.6 0.7 constant_dynamic-update-slice_fusion.9
  107.3 0.7 constant_dynamic-update-slice_fusion.8
  108.0 0.7 constant_dynamic-update-slice_fusion.7
  108.7 0.7 constant_dynamic-update-slice_fusion.6
  109.4 0.7 constant_dynamic-update-slice_fusion.5
  110.1 0.7 constant_dynamic-update-slice_fusion.4
  110.8 0.7 constant_dynamic-update-slice_fusion.3
  111.5 0.7 constant_dynamic-update-slice_fusion.2
  112.2 0.7 constant_dynamic-update-slice_fusion.1
  112.9 0.7 constant_dynamic-update-slice_fusion
  113.6 11.4 %all_to_all.5 = f32[16,1,2,8,128]{4,3,2,1,0:T(8,128)S(1)} all-to-all(f32[16,1,2,8,128]{4,3,2,1,0:T(8,128)S(1)} %constant_dynamic-update-slice_fusion), channel_id=1, replica_groups=mesh['grp'=2,'row'=16] {'row'}, dimensions={0} | all-to-all | bytes 262144 | tf_op jit(solution)/shard_map/all_to_all | solution.py:38
  124.9 0.7 slice_bitcast_fusion
  (4 shorter events, 0.0 us)
Async XLA Ops:
  7.2 28.3 %copy-start = (f32[24,128,128]{2,1,0:T(8,128)S(1)}, f32[24,128,128]{2,1,0:T(8,128)}, u32[]{:S(2)}) copy-start(f32[24,128,128]{2,1,0:T(8,128)} %param.8) | copy-start | bytes 4718596
  7.2 95.2 %reduce-scatter.2.cloned.1.call-start = ((), (), s32[]{:S(2)}) async-start(), calls=%async_computation.2 | async-start | bytes 2228224 | tf_op jit(solution)/shard_map/reduce_scatter | solution.py:36
  35.4 1.9 %copy-start.1 = (f32[24,128,128]{2,1,0:T(8,128)S(1)}, f32[24,128,128]{2,1,0:T(8,128)}, u32[]{:S(2)}) copy-start(f32[24,128,128]{2,1,0:T(8,128)} %param.9) | copy-start | bytes 4718596
Sparse Core Ops, SparseCore 0:
  43.3 59.0 reduce-scatter.1
